TPU v7x, 32 devices: a whole 2x2x4 slice. The times are simulated.
32 devices in a mesh: aa: 8 (over z, y), ba: 4 (over x, core).
Axes of the slice: x: 2, y: 2, z: 4, core: 2. Of those that a mesh axis runs over, the one named last changes fastest.
Arguments:
- tokens: bfloat16 [4096, 8192], P('aa', 'ba'), may hold values from -6 to 6
- request_adapter_index: int32 [4096, 1], P('aa'), may hold values from 0 to 127; in each aligned block of 512 rows (0 to 511, 512 to 1023, ...) at most 8 rows name the same one
- key_weight: bfloat16 [8192, 1024], P('ba'), may hold values from -0.0625 to 0.0625
- value_weight: bfloat16 [8192, 1024], P('ba'), may hold values from -0.0625 to 0.0625
- adapter_down_weight: bfloat16 [128, 32, 8192], P('aa', None, 'ba'), may hold values from -0.0625 to 0.0625
- adapter_up_weight: bfloat16 [128, 2, 16, 1024], P('aa'), may hold values from -1.5 to 1.5
Outputs:
- keys_out: bfloat16 [4096, 1024], P('aa', 'ba')
- values_out: bfloat16 [4096, 1024], P('aa', 'ba')
Inputs may be any that keep to these rules, and one draw needn't show every extreme that they name: `request_adapter_index`: among the 512 rows of one device no adapter is named more than 8 times, a bound that some block reaches.
All inputs are finite; a program needn't handle non-finite values.
Results may differ from a plain program's by a relative error of at most 0.001.
Values may be sent and summed in bfloat16 or wider, within the bound.
A program may use at most 128 MiB of HBM per device.

v0:
```python
import jax
import jax.numpy as jnp
from jax import lax
from jax.sharding import PartitionSpec as P


def on_device(
    tokens, request_adapter_index, key_weight, value_weight, adapter_down_weight, adapter_up_weight
):
    bank_count = lax.axis_size("aa")
    split_count = lax.axis_size("ba")
    tok_rows, width_local = tokens.shape
    resident_adapters, twice_rank, spare_width = adapter_down_weight.shape
    rank_width = twice_rank // 2
    kv_width = key_weight.shape[1]
    kv_local = kv_width // split_count
    adapters_all = resident_adapters * bank_count
    capacity = max(2, 2 * tok_rows // adapters_all)
    slot_total = adapters_all * capacity
    selected_adapter = request_adapter_index[:, 0]
    positions = jnp.arange(tok_rows, dtype=jnp.int32)
    same_adapter = (selected_adapter[:, None] == selected_adapter[None, :]) & (
        positions[None, :] < positions[:, None]
    )
    earlier = jnp.sum(same_adapter.astype(jnp.int32), axis=1)
    slot_of = selected_adapter * capacity + earlier
    source = jnp.zeros((slot_total,), jnp.int32).at[slot_of].set(positions)
    outgoing = tokens[source].reshape(bank_count, resident_adapters, capacity, width_local)
    complete_up_weight = adapter_up_weight.astype(jnp.float32)
    offset = lax.axis_index("ba") * kv_local
    up_used = lax.dynamic_slice_in_dim(complete_up_weight, offset, kv_local, 3)
    partial_rank = jnp.einsum(
        "sakd,ajd->sakj",
        lax.all_to_all(outgoing, "aa", split_axis=0, concat_axis=0, tiled=True),
        adapter_down_weight,
        preferred_element_type=jnp.float32,
    )
    rank_sum = lax.psum(partial_rank, "ba")
    key_change = jnp.einsum(
        "sakr,arc->sakc", rank_sum[..., :rank_width], up_used[:, 0], precision=lax.Precision.HIGHEST
    )
    value_change = jnp.einsum(
        "sakr,arc->sakc", rank_sum[..., rank_width:], up_used[:, 1], precision=lax.Precision.HIGHEST
    )
    key_change, value_change = (key_change, value_change)
    changes = jnp.concatenate([key_change, value_change], axis=3)
    returned = lax.all_to_all(changes, "aa", split_axis=0, concat_axis=0, tiled=True)
    per_token = returned.reshape(slot_total, returned.shape[3])[slot_of]
    key_part = jnp.dot(tokens, key_weight, preferred_element_type=jnp.float32)
    value_part = jnp.dot(tokens, value_weight, preferred_element_type=jnp.float32)
    base_part = jnp.stack(
        [
            key_part.reshape(tok_rows, split_count, kv_local),
            value_part.reshape(tok_rows, split_count, kv_local),
        ],
        axis=2,
    )
    base_part = base_part.reshape(tok_rows, 2 * kv_width)
    summed = lax.psum_scatter(base_part, "ba", scatter_dimension=1, tiled=True) + per_token
    return (summed[:, :kv_local].astype(jnp.bfloat16), summed[:, kv_local:].astype(jnp.bfloat16))


def solution(mesh):
    return jax.shard_map(
        on_device,
        mesh=mesh,
        in_specs=(
            P("aa", "ba"),
            P("aa", None),
            P("ba", None),
            P("ba", None),
            P("aa", None, "ba"),
            P("aa", None, None, None),
        ),
        out_specs=(P("aa", "ba"), P("aa", "ba")),
        check_vma=False,
    )
```

profile of v0, /device:TPU:0, one launch (start us, length us, event | category | flops | bytes accessed | tf_op | source)
XLA Modules:
  0.0 226.5 jit_solution(3691659439120171811)
XLA Ops:
  7.2 1.1 convert_reduce_fusion
  8.3 0.7 compare_select_fusion
  9.0 2.4 %scatter_custom_fusion = s32[1024]{0:T(1024)S(1)} fusion(s32[512]{0:T(512)S(1)} %bitcast.40, s32[512]{0:T(512)S(1)} %iota.9, s32[]{:T(128)} %constant.6.clone.1), kind=kCustom, calls=%fused_computation.23 | custom fusion | bytes 4100 | tf_op jit(solution)/shard_map/scatter | solution.py:27
  11.4 6.0 %gather_fusion = bf16[1024,2048]{1,0:T(8,128)(2,1)} fusion(bf16[512,2048]{1,0:T(8,128)(2,1)S(1)} %copy-done, s32[1024]{0:T(1024)S(1)} %fusion.11), kind=kCustom, calls=%fused_computation | custom fusion | bytes 8392704 | tf_op jit(solution)/shard_map/gather | solution.py:28
  17.5 7.3 %all-to-all-start = ((bf16[8,16,8,2048]{3,2,1,0:T(8,128)(2,1)}), bf16[8,16,8,2048]{3,2,1,0:T(8,128)(2,1)}, u32[]{:S(2)}, u32[]{:S(2)}) async-start(bf16[8,16,8,2048]{3,2,1,0:T(8,128)(2,1)} %bitcast.38), calls=%async_computation.1 | async-start | bytes 8388608 | tf_op jit(solution)/shard_map/all_to_all | solution.py:34
  24.8 5.8 %fusion.17 = f32[512,1024]{1,0:T(8,128)} fusion(bf16[512,2048]{1,0:T(8,128)(2,1)S(1)} %copy-done, bf16[2048,1024]{1,0:T(8,128)(2,1)} %param.8), kind=kOutput, calls=%fused_computation.28 | convolution fusion | flops 2147483648 | bytes 8388608 | tf_op jit(solution)/shard_map/dot_general | solution.py:49
  30.6 3.1 %stack_reshape.6 = f32[512,4,1,256]{3,1,0,2:T(4,128)} reshape(f32[512,1024]{1,0:T(8,128)} %fusion.17) | data formatting | bytes 4194304 | tf_op jit(solution)/shard_map/stack;reshape | solution.py:51
  33.8 5.9 %fusion.18 = f32[512,1024]{1,0:T(8,128)} fusion(bf16[512,2048]{1,0:T(8,128)(2,1)S(1)} %copy-done, bf16[2048,1024]{1,0:T(8,128)(2,1)} %param.9), kind=kOutput, calls=%fused_computation.29 | convolution fusion | flops 2147483648 | bytes 8388608 | tf_op jit(solution)/shard_map/dot_general | solution.py:50
  39.6 3.2 %stack_reshape.7 = f32[512,4,1,256]{3,1,0,2:T(4,128)} reshape(f32[512,1024]{1,0:T(8,128)} %fusion.18) | data formatting | bytes 4194304 | tf_op jit(solution)/shard_map/stack;reshape | solution.py:51
  42.8 75.3 %all-to-all-done = bf16[8,16,8,2048]{3,2,1,0:T(8,128)(2,1)} async-done(((bf16[8,16,8,2048]{3,2,1,0:T(8,128)(2,1)}), bf16[8,16,8,2048]{3,2,1,0:T(8,128)(2,1)}, u32[]{:S(2)}, u32[]{:S(2)}) %all-to-all-start) | async-done | bytes 4194336 | tf_op jit(solution)/shard_map/all_to_all | solution.py:34
  118.1 4.9 %fusion.3 = f32[8,16,8,32]{3,2,0,1:T(8,128)} fusion(bf16[16,32,2048]{2,1,0:T(8,128)(2,1)} %param.10, bf16[8,16,8,2048]{3,2,1,0:T(8,128)(2,1)} %all-to-all-done), kind=kOutput, calls=%fused_computation.10 | convolution fusion | flops 134217728 | bytes 6422528 | tf_op jit(solution)/shard_map/sakd,ajd->sakj/dot_general | solution.py:32
  123.2 3.2 %pad_maximum_fusion = f32[512,4,2,256]{3,1,0,2:T(4,128)S(1)} fusion(f32[512,4,1,256]{3,1,0,2:T(4,128)} %stack_reshape.7, f32[512,4,1,256]{3,1,0,2:T(4,128)} %stack_reshape.6), kind=kLoop, calls=%fused_computation.3 | loop fusion | flops 1048576 | bytes 8388608 | tf_op jit(solution)/shard_map/stack | solution.py:51
  126.4 5.2 %copy.18 = f32[512,4,2,256]{3,2,1,0:T(2,128)} copy(f32[512,4,2,256]{3,1,0,2:T(4,128)S(1)} %pad_maximum_fusion) | data formatting | bytes 8388608 | tf_op jit(solution)/shard_map/stack | solution.py:51
  131.6 6.4 %reshape.15 = f32[512,2048]{1,0:T(8,128)} reshape(f32[512,4,2,256]{3,2,1,0:T(2,128)} %copy.18) | data formatting | bytes 8388608 | tf_op jit(solution)/shard_map/reshape | solution.py:58
  138.1 17.5 %all-reduce.2.cloned.1.call-done = f32[8,16,8,32]{3,2,0,1:T(8,128)} async-done(((f32[8,16,8,32]{3,2,0,1:T(8,128)}), f32[8,16,8,32]{3,2,0,1:T(8,128)}) %all-reduce.2.cloned.1.call-update) | async-done | bytes 131088 | tf_op jit(solution)/shard_map/psum | solution.py:38
  155.6 1.7 convolution_bitcast_fusion.1
  157.3 1.8 convolution_bitcast_fusion
  159.1 0.3 pad_maximum_fusion.1
  159.4 1.5 copy.21
  160.9 5.5 %all-to-all-start.1 = ((f32[8,16,8,512]{3,2,1,0:T(8,128)}), f32[8,16,8,512]{3,2,1,0:T(8,128)}, u32[]{:S(2)}, u32[]{:S(2)}) async-start(f32[8,16,8,512]{3,2,1,0:T(8,128)} %copy.21), calls=%async_computation.2 | async-start | bytes 4194304 | tf_op jit(solution)/shard_map/all_to_all | solution.py:47
  166.4 47.4 %all-to-all-done.1 = f32[8,16,8,512]{3,2,1,0:T(8,128)} async-done(((f32[8,16,8,512]{3,2,1,0:T(8,128)}), f32[8,16,8,512]{3,2,1,0:T(8,128)}, u32[]{:S(2)}, u32[]{:S(2)}) %all-to-all-start.1) | async-done | bytes 2097184 | tf_op jit(solution)/shard_map/all_to_all | solution.py:47
  213.8 3.6 %gather_fusion.1 = f32[512,512]{1,0:T(8,128)S(1)} fusion(f32[1024,512]{1,0:T(8,128)} %bitcast.15, s32[1024]{0:T(1024)S(1)} %pad_clamp_fusion), kind=kCustom, calls=%fused_computation.1 | custom fusion | bytes 2099200 | tf_op jit(solution)/shard_map/gather | solution.py:48
  217.4 1.4 add_convert_fusion
  218.8 0.8 fusion.16
  (10 shorter events, 0.3 us)
Async XLA Ops:
  7.2 4.3 %copy-start = (bf16[512,2048]{1,0:T(8,128)(2,1)S(1)}, bf16[512,2048]{1,0:T(8,128)(2,1)}, u32[]{:S(2)}) copy-start(bf16[512,2048]{1,0:T(8,128)(2,1)} %param.6) | copy-start | bytes 6291460
  17.5 100.6 %all-to-all-start = ((bf16[8,16,8,2048]{3,2,1,0:T(8,128)(2,1)}), bf16[8,16,8,2048]{3,2,1,0:T(8,128)(2,1)}, u32[]{:S(2)}, u32[]{:S(2)}) async-start(bf16[8,16,8,2048]{3,2,1,0:T(8,128)(2,1)} %bitcast.38), calls=%async_computation.1 | async-start | bytes 8388608 | tf_op jit(solution)/shard_map/all_to_all | solution.py:34
  24.8 130.9 %all-reduce.2.cloned.1.call-start = ((), (), s32[]{:S(2)}) async-start(), calls=%async_computation.4 | async-start | bytes 1048576 | tf_op jit(solution)/shard_map/psum | solution.py:38
  123.0 94.4 %reduce-scatter.2.cloned.1.call-start = ((), (), s32[]{:S(2)}) async-start(), calls=%async_computation.3 | async-start | bytes 5242880 | tf_op jit(solution)/shard_map/reduce_scatter | solution.py:59
  160.9 52.9 %all-to-all-start.1 = ((f32[8,16,8,512]{3,2,1,0:T(8,128)}), f32[8,16,8,512]{3,2,1,0:T(8,128)}, u32[]{:S(2)}, u32[]{:S(2)}) async-start(f32[8,16,8,512]{3,2,1,0:T(8,128)} %copy.21), calls=%async_computation.2 | async-start | bytes 4194304 | tf_op jit(solution)/shard_map/all_to_all | solution.py:47
Sparse Core Ops, SparseCore 0:
  123.1 32.4 all-reduce.1
  158.2 44.5 reduce-scatter.1
where the time goes:
time: 227 us; the launch traced here: 226 us
  waiting for transfers between devices  140 us (62%)
  local copies, waits for them, and re-layouts  32.4 us (14%)
  matrix products  20 us (9%)
  between operations  14.1 us (6%)
  starting transfers between devices  13.1 us (6%)
  other arithmetic  6.65 us (3%)
    all_to_all x1, waiting for transfers between devices, on_device(): lax.all_to_all(outgoing, 'aa', split_axis=0, concat_axis=0, tiled=True)  75.3 us
    all_to_all x1, waiting for transfers between devices, on_device(): lax.all_to_all(changes, 'aa', split_axis=0, concat_axis=0, tiled=True)  47.4 us
    psum x1, waiting for transfers between devices, on_device(): rank_sum = lax.psum(partial_rank, 'ba')  17.5 us
    another operation x3, local copies, waits for them, and re-layouts, on_device(): jnp.stack([key_part.reshape(tok_rows, split_count, kv_local), value_part....  11.5 us
    all_to_all x1, starting transfers between devices, on_device(): lax.all_to_all(outgoing, 'aa', split_axis=0, concat_axis=0, tiled=True)  7.31 us
    reshape x1, local copies, waits for them, and re-layouts, on_device(): base_part = base_part.reshape(tok_rows, 2 * kv_width)  6.43 us
    gather x1, local copies, waits for them, and re-layouts, on_device(): tokens[source].reshape(bank_count, resident_adapters, capacity, width_local)  6.02 us
    dot_general x1, matrix products, on_device(): jnp.dot(tokens, value_weight, preferred_element_type=jnp.float32)  5.85 us
  transfers between devices with their start and end apart: 4, of which 3 were waited for; matrix products, arithmetic and copies ran while one was open for 18% of the time, Pallas kernels for 0%

commit v1 on v0

--- a/solution.py
+++ b/solution.py
@@ -35,7 +35,8 @@
         adapter_down_weight,
         preferred_element_type=jnp.float32,
     )
-    rank_sum = lax.psum(partial_rank, "ba")
+    parts = lax.all_gather(partial_rank, "ba")
+    rank_sum = jnp.sum(parts, axis=0)
     key_change = jnp.einsum(
         "sakr,arc->sakc", rank_sum[..., :rank_width], up_used[:, 0], precision=lax.Precision.HIGHEST
     )

time: 227 us -> 212 us (0.934)
  waiting for transfers between devices: 140 us -> 109 us
  blocking collectives: 0 us -> 16.3 us
    psum x1 -> x0, waiting for transfers between devices: 17.5 us -> none  [on_device(): rank_sum = lax.psum(partial_rank, 'ba')]
    all_gather x0 -> x1, blocking collectives: none -> 16.3 us  [on_device(): parts = lax.all_gather(partial_rank, 'ba')]
    all_to_all x1, waiting for transfers between devices: 75.3 us -> 60.4 us  [on_device(): lax.all_to_all(outgoing, 'aa', split_axis=0, concat_axis=0, tiled=True)]
  transfers between devices with their start and end apart: 4 -> 3, of which waited for: 3 -> 2; matrix products, arithmetic and copies ran while one was open for 18% -> 22% of each run, Pallas kernels for 0% -> 0%
where the time goes in v1:
time: 212 us; the launch traced here: 211 us
  waiting for transfers between devices  109 us (51%)
  local copies, waits for them, and re-layouts  32.3 us (15%)
  matrix products  18.8 us (9%)
  blocking collectives  16.3 us (8%)
  between operations  14.1 us (7%)
  starting transfers between devices  11.7 us (6%)
  other arithmetic  8.52 us (4%)
    all_to_all x1, waiting for transfers between devices, on_device(): lax.all_to_all(outgoing, 'aa', split_axis=0, concat_axis=0, tiled=True)  60.4 us
    all_to_all x1, waiting for transfers between devices, on_device(): lax.all_to_all(changes, 'aa', split_axis=0, concat_axis=0, tiled=True)  49 us
    all_gather x1, blocking collectives, on_device(): parts = lax.all_gather(partial_rank, 'ba')  16.3 us
    another operation x3, local copies, waits for them, and re-layouts, on_device(): jnp.stack([key_part.reshape(tok_rows, split_count, kv_local), value_part....  11.5 us
    all_to_all x1, starting transfers between devices, on_device(): lax.all_to_all(outgoing, 'aa', split_axis=0, concat_axis=0, tiled=True)  7.31 us
    reshape x1, local copies, waits for them, and re-layouts, on_device(): base_part = base_part.reshape(tok_rows, 2 * kv_width)  6.4 us
    gather x1, local copies, waits for them, and re-layouts, on_device(): tokens[source].reshape(bank_count, resident_adapters, capacity, width_local)  6.03 us
    dot_general x1, matrix products, on_device(): jnp.dot(tokens, value_weight, preferred_element_type=jnp.float32)  5.88 us
  transfers between devices with their start and end apart: 3, of which 2 were waited for; matrix products, arithmetic and copies ran while one was open for 22% of the time, Pallas kernels for 0%

profile of v1, /device:TPU:0, one launch (start us, length us, event | category | flops | bytes accessed | tf_op | source)
XLA Modules:
  0.0 211.3 jit_solution(10746339586685548084)
XLA Ops:
  7.2 1.1 convert_reduce_fusion
  8.3 0.7 compare_select_fusion
  9.0 2.4 %scatter_custom_fusion = s32[1024]{0:T(1024)S(1)} fusion(s32[512]{0:T(512)S(1)} %bitcast.42, s32[512]{0:T(512)S(1)} %iota.9, s32[]{:T(128)} %constant.7.clone.1), kind=kCustom, calls=%fused_computation.23 | custom fusion | bytes 4100 | tf_op jit(solution)/shard_map/scatter | solution.py:27
  11.4 6.0 %gather_fusion = bf16[1024,2048]{1,0:T(8,128)(2,1)} fusion(bf16[512,2048]{1,0:T(8,128)(2,1)S(1)} %copy-done, s32[1024]{0:T(1024)S(1)} %fusion.11), kind=kCustom, calls=%fused_computation | custom fusion | bytes 8392704 | tf_op jit(solution)/shard_map/gather | solution.py:28
  17.5 7.3 %all-to-all-start = ((bf16[8,16,8,2048]{3,2,1,0:T(8,128)(2,1)}), bf16[8,16,8,2048]{3,2,1,0:T(8,128)(2,1)}, u32[]{:S(2)}, u32[]{:S(2)}) async-start(bf16[8,16,8,2048]{3,2,1,0:T(8,128)(2,1)} %bitcast.39), calls=%async_computation.1 | async-start | bytes 8388608 | tf_op jit(solution)/shard_map/all_to_all | solution.py:34
  24.8 5.8 %fusion.17 = f32[512,1024]{1,0:T(8,128)} fusion(bf16[512,2048]{1,0:T(8,128)(2,1)S(1)} %copy-done, bf16[2048,1024]{1,0:T(8,128)(2,1)} %param.8), kind=kOutput, calls=%fused_computation.28 | convolution fusion | flops 2147483648 | bytes 8388608 | tf_op jit(solution)/shard_map/dot_general | solution.py:50
  30.6 3.2 %stack_reshape.6 = f32[512,4,1,256]{3,1,0,2:T(4,128)} reshape(f32[512,1024]{1,0:T(8,128)} %fusion.17) | data formatting | bytes 4194304 | tf_op jit(solution)/shard_map/stack;reshape | solution.py:52
  33.8 5.9 %fusion.18 = f32[512,1024]{1,0:T(8,128)} fusion(bf16[512,2048]{1,0:T(8,128)(2,1)S(1)} %copy-done, bf16[2048,1024]{1,0:T(8,128)(2,1)} %param.9), kind=kOutput, calls=%fused_computation.29 | convolution fusion | flops 2147483648 | bytes 8388608 | tf_op jit(solution)/shard_map/dot_general | solution.py:51
  39.7 3.2 %stack_reshape.7 = f32[512,4,1,256]{3,1,0,2:T(4,128)} reshape(f32[512,1024]{1,0:T(8,128)} %fusion.18) | data formatting | bytes 4194304 | tf_op jit(solution)/shard_map/stack;reshape | solution.py:52
  42.8 3.2 %pad_maximum_fusion = f32[512,4,2,256]{3,1,0,2:T(4,128)S(1)} fusion(f32[512,4,1,256]{3,1,0,2:T(4,128)} %stack_reshape.7, f32[512,4,1,256]{3,1,0,2:T(4,128)} %stack_reshape.6), kind=kLoop, calls=%fused_computation.3 | loop fusion | flops 1048576 | bytes 8388608 | tf_op jit(solution)/shard_map/stack | solution.py:52
  46.0 5.2 %copy.18 = f32[512,4,2,256]{3,2,1,0:T(2,128)} copy(f32[512,4,2,256]{3,1,0,2:T(4,128)S(1)} %pad_maximum_fusion) | data formatting | bytes 8388608 | tf_op jit(solution)/shard_map/stack | solution.py:52
  51.2 6.4 %reshape.15 = f32[512,2048]{1,0:T(8,128)} reshape(f32[512,4,2,256]{3,2,1,0:T(2,128)} %copy.18) | data formatting | bytes 8388608 | tf_op jit(solution)/shard_map/reshape | solution.py:59
  57.6 60.4 %all-to-all-done = bf16[8,16,8,2048]{3,2,1,0:T(8,128)(2,1)} async-done(((bf16[8,16,8,2048]{3,2,1,0:T(8,128)(2,1)}), bf16[8,16,8,2048]{3,2,1,0:T(8,128)(2,1)}, u32[]{:S(2)}, u32[]{:S(2)}) %all-to-all-start) | async-done | bytes 4194336 | tf_op jit(solution)/shard_map/all_to_all | solution.py:34
  118.1 4.1 %fusion.3 = f32[8,16,8,32]{3,2,0,1:T(8,128)S(1)} fusion(bf16[16,32,2048]{2,1,0:T(8,128)(2,1)} %param.10, bf16[8,16,8,2048]{3,2,1,0:T(8,128)(2,1)} %all-to-all-done), kind=kOutput, calls=%fused_computation.10 | convolution fusion | flops 134217728 | bytes 6422528 | tf_op jit(solution)/shard_map/sakd,ajd->sakj/dot_general | solution.py:32
  122.2 16.3 %all-gather = f32[32,16,8,32]{3,2,0,1:T(8,128)} all-gather(f32[8,16,8,32]{3,2,0,1:T(8,128)S(1)} %fusion.3), channel_id=2, replica_groups=mesh['aa'=8,'ba'=4] {'ba'}, dimensions={0}, use_global_device_ids=true | all-gather | bytes 655360 | tf_op jit(solution)/shard_map/all_gather | solution.py:38
  138.5 1.9 reduce_sum.22
  140.4 1.5 convolution_bitcast_fusion.1
  141.9 1.5 convolution_bitcast_fusion
  143.7 1.5 copy.21
  145.2 4.3 %all-to-all-start.1 = ((f32[8,16,8,512]{3,2,1,0:T(8,128)}), f32[8,16,8,512]{3,2,1,0:T(8,128)}, u32[]{:S(2)}, u32[]{:S(2)}) async-start(f32[8,16,8,512]{3,2,1,0:T(8,128)} %copy.21), calls=%async_computation.2 | async-start | bytes 4194304 | tf_op jit(solution)/shard_map/all_to_all | solution.py:48
  149.5 49.0 %all-to-all-done.1 = f32[8,16,8,512]{3,2,1,0:T(8,128)} async-done(((f32[8,16,8,512]{3,2,1,0:T(8,128)}), f32[8,16,8,512]{3,2,1,0:T(8,128)}, u32[]{:S(2)}, u32[]{:S(2)}) %all-to-all-start.1) | async-done | bytes 2097184 | tf_op jit(solution)/shard_map/all_to_all | solution.py:48
  198.6 3.6 %gather_fusion.1 = f32[512,512]{1,0:T(8,128)S(1)} fusion(f32[1024,512]{1,0:T(8,128)} %bitcast.16, s32[1024]{0:T(1024)S(1)} %pad_clamp_fusion), kind=kCustom, calls=%fused_computation.1 | custom fusion | bytes 2099200 | tf_op jit(solution)/shard_map/gather | solution.py:49
  202.2 1.4 add_convert_fusion
  203.6 0.8 fusion.16
  (9 shorter events, 0.4 us)
Async XLA Ops:
  7.2 4.3 %copy-start = (bf16[512,2048]{1,0:T(8,128)(2,1)S(1)}, bf16[512,2048]{1,0:T(8,128)(2,1)}, u32[]{:S(2)}) copy-start(bf16[512,2048]{1,0:T(8,128)(2,1)} %param.6) | copy-start | bytes 6291460
  17.5 100.6 %all-to-all-start = ((bf16[8,16,8,2048]{3,2,1,0:T(8,128)(2,1)}), bf16[8,16,8,2048]{3,2,1,0:T(8,128)(2,1)}, u32[]{:S(2)}, u32[]{:S(2)}) async-start(bf16[8,16,8,2048]{3,2,1,0:T(8,128)(2,1)} %bitcast.39), calls=%async_computation.1 | async-start | bytes 8388608 | tf_op jit(solution)/shard_map/all_to_all | solution.py:34
  24.8 177.4 %reduce-scatter.2.cloned.1.call-start = ((), (), s32[]{:S(2)}) async-start(), calls=%async_computation.3 | async-start | bytes 5242880 | tf_op jit(solution)/shard_map/reduce_scatter | solution.py:60
  145.2 53.4 %all-to-all-start.1 = ((f32[8,16,8,512]{3,2,1,0:T(8,128)}), f32[8,16,8,512]{3,2,1,0:T(8,128)}, u32[]{:S(2)}, u32[]{:S(2)}) async-start(f32[8,16,8,512]{3,2,1,0:T(8,128)} %copy.21), calls=%async_computation.2 | async-start | bytes 4194304 | tf_op jit(solution)/shard_map/all_to_all | solution.py:48
Sparse Core Ops, SparseCore 0:
  57.8 45.7 reduce-scatter.1
